TPU v7x, 32 devices: a whole 2x2x4 slice. The times are simulated.
32 devices in a mesh: ga: 8 (over z, y), ba: 4 (over x, core).
Axes of the slice: x: 2, y: 2, z: 4, core: 2. Of those that a mesh axis runs over, the one named last changes fastest.
Arguments:
- coefficients: bfloat16 [10240, 6144], P('ga', 'ba')
- rotation: bfloat16 [6144, 6144], P('ga', 'ba'), may hold values from -0.078125 to 0.078125
Outputs:
- new_coefficients: bfloat16 [10240, 6144], P('ga', 'ba')
- band_rms: float32 [6144], P('ba')
All inputs are finite; a program needn't handle non-finite values.
Results may differ from a plain program's by a relative error of at most 0.0004.
Values may be sent and summed in bfloat16 or wider, within the bound.
A program may use at most 128 MiB of HBM per device.

v0:
```python
import jax
import jax.numpy as jnp
from jax import lax
from jax.sharding import PartitionSpec as P


def body(coefficients, rotation):
    all_bands = lax.all_gather(coefficients, "ba", axis=1, tiled=True)
    rotated = jnp.dot(
        all_bands,
        lax.all_gather(rotation, "ga", axis=0, tiled=True),
        preferred_element_type=jnp.float32,
    )
    squares = lax.psum(jnp.sum(rotated * rotated, axis=0), "ga")
    total_rows = coefficients.shape[0] * lax.axis_size("ga")
    band_rms = jnp.sqrt(squares / total_rows + 1e-06)
    return ((rotated / band_rms).astype(jnp.bfloat16), band_rms)


def solution(mesh):
    in_specs = (P("ga", "ba"), P("ga", "ba"))
    out_specs = (P("ga", "ba"), P("ba"))
    return jax.shard_map(body, mesh=mesh, in_specs=in_specs, out_specs=out_specs, check_vma=False)
```

profile of v0, /device:TPU:0, one launch (start us, length us, event | category | flops | bytes accessed | tf_op | source)
XLA Modules:
  0.0 543.6 jit_solution(14183646409815637874)
XLA Ops:
  7.2 0.0 all-gather.3.cloned.1.call-start
  7.2 0.7 all-gather.3.cloned.1.call-update
  7.9 0.0 all-gather.5.cloned.1.call-start
  7.9 0.7 all-gather.5.cloned.1.call-update
  8.6 103.6 %all-gather.3.cloned.1.call-done = bf16[1280,6144]{1,0:T(8,128)(2,1)} async-done(((bf16[1280,1536]{1,0:T(8,128)(2,1)}), bf16[1280,6144]{1,0:T(8,128)(2,1)}) %all-gather.3.cloned.1.call-update) | async-done | bytes 15728656 | tf_op jit(solution)/shard_map/all_gather | solution.py:8
  112.2 364.0 %all-gather.5.cloned.1.call-done = bf16[6144,1536]{1,0:T(8,128)(2,1)} async-done(((bf16[768,1536]{1,0:T(8,128)(2,1)}), bf16[6144,1536]{1,0:T(8,128)(2,1)}) %all-gather.5.cloned.1.call-update) | async-done | bytes 18874384 | tf_op jit(solution)/shard_map/all_gather | solution.py:11
  476.2 33.9 %multiply_reduce_fusion = (f32[1536]{0:T(1024)S(1)}, f32[1280,1536]{1,0:T(8,128)}) fusion(bf16[1280,6144]{1,0:T(8,128)(2,1)} %all-gather.3.cloned.1.call-done, bf16[6144,1536]{1,0:T(8,128)(2,1)} %all-gather.5.cloned.1.call-done), kind=kOutput, calls=%fused_computation.1 | convolution fusion | flops 24163121152 | bytes 42473472 | tf_op jit(solution)/shard_map/dot_general | solution.py:9
  510.1 20.4 %psum.7 = f32[1536]{0:T(1024)S(1)} all-reduce(f32[1536]{0:T(1024)S(1)} %get-tuple-element.2), channel_id=1, replica_groups=mesh['ga'=8,'ba'=4] {'ga'}, use_global_device_ids=true, to_apply=%region_1.0 | all-reduce | flops 1536 | bytes 12288 | tf_op jit(solution)/shard_map/psum | solution.py:14
  530.6 0.0 copy-start
  530.6 6.2 %divide_convert_fusion = bf16[1280,1536]{1,0:T(8,128)(2,1)} fusion(f32[1280,1536]{1,0:T(8,128)} %get-tuple-element.3, f32[1536]{0:T(1024)S(1)} %add_sqrt_fusion), kind=kLoop, calls=%fused_computation | loop fusion | flops 3932160 | bytes 11802624 | tf_op jit(solution)/shard_map/convert_element_type | solution.py:17
  536.8 0.0 copy-done
  (1 shorter events, 0.0 us)
Async XLA Ops:
  7.2 105.1 %all-gather.3.cloned.1.call-start = ((), (), s32[]{:S(2)}) async-start(), calls=%async_computation | async-start | bytes 19660800 | tf_op jit(solution)/shard_map/all_gather | solution.py:8
  7.9 468.3 %all-gather.5.cloned.1.call-start = ((), (), s32[]{:S(2)}) async-start(), calls=%async_computation.1 | async-start | bytes 21233664 | tf_op jit(solution)/shard_map/all_gather | solution.py:11
  530.6 6.2 %copy-start = (f32[1536]{0:T(1024)}, f32[1536]{0:T(1024)S(1)}, u32[]{:S(2)}) copy-start(f32[1536]{0:T(1024)S(1)} %add_sqrt_fusion) | copy-start | bytes 18436
Sparse Core Ops, SparseCore 0:
  9.5 102.6 all-gather.2
  113.8 362.3 all-gather.4
where the time goes:
time: 544 us
  waiting for transfers between devices  469 us (86%)
  matrix products  33.9 us (6%)
  blocking collectives  20.4 us (4%)
  between operations  14.1 us (3%)
  other arithmetic  6.19 us (1%)
    all_gather x1, waiting for transfers between devices, body(): lax.all_gather(rotation, 'ga', axis=0, tiled=True)  364 us
    all_gather x1, waiting for transfers between devices, body(): all_bands = lax.all_gather(coefficients, 'ba', axis=1, tiled=True)  104 us
    dot_general x1, matrix products, body(): jnp.dot(all_bands, lax.all_gather(rotation, 'ga', axis=0, tiled=True), pr...  33.9 us
    psum x1, blocking collectives, body(): squares = lax.psum(jnp.sum(rotated * rotated, axis=0), 'ga')  20.4 us
  transfers between devices with their start and end apart: 2, of which 2 were waited for; matrix products, arithmetic and copies ran while one was open for 0% of the time, Pallas kernels for 0%

commit v1 on v0

--- a/solution.py
+++ b/solution.py
@@ -4,8 +4,19 @@
 from jax.sharding import PartitionSpec as P
 
 
+def turned_line(x, name, d):
+    count = lax.axis_size(name)
+    right = [(i, (i + 1) % count) for i in range(count)]
+    parts = [x]
+    for far in range(1, count):
+        parts = [lax.ppermute(parts[0], name, right), *parts]
+    whole = jnp.concatenate(parts, axis=d)
+    shift = (lax.axis_index(name) + 1) * parts[-1].shape[d]
+    return jnp.roll(whole, shift, axis=d)
+
+
 def body(coefficients, rotation):
-    all_bands = lax.all_gather(coefficients, "ba", axis=1, tiled=True)
+    all_bands = turned_line(coefficients, "ba", 1)
     rotated = jnp.dot(
         all_bands,
         lax.all_gather(rotation, "ga", axis=0, tiled=True),

time: 544 us -> 443 us (0.81)
  waiting for transfers between devices: 469 us -> 336 us
  local copies, waits for them, and re-layouts: 0.01 us -> 30.4 us
    all_gather x1, waiting for transfers between devices: 364 us -> 200 us  [body(): lax.all_gather(rotation, 'ga', axis=0, tiled=True)]
    ppermute x0 -> x3, waiting for transfers between devices: none -> 136 us  [turned_line(): parts = [lax.ppermute(parts[0], name, right), *parts]]
    all_gather x1 -> x0, waiting for transfers between devices: 104 us -> none  [body(): all_bands = lax.all_gather(coefficients, 'ba', axis=1, tiled=True)]
    unnamed x2 -> x15, local copies, waits for them, and re-layouts: 0.01 us -> 28.3 us
  transfers between devices with their start and end apart: 2 -> 4, of which waited for: 2 -> 4; matrix products, arithmetic and copies ran while one was open for 0% -> 6% of each run, Pallas kernels for 0% -> 0%
where the time goes in v1:
time: 443 us; the launch traced here: 442 us
  waiting for transfers between devices  336 us (76%)
  matrix products  34.3 us (8%)
  local copies, waits for them, and re-layouts  30.4 us (7%)
  blocking collectives  20.4 us (5%)
  between operations  14.1 us (3%)
  other arithmetic  6.19 us (1%)
    all_gather x1, waiting for transfers between devices, body(): lax.all_gather(rotation, 'ga', axis=0, tiled=True)  200 us
    ppermute x3, waiting for transfers between devices, turned_line(): parts = [lax.ppermute(parts[0], name, right), *parts]  136 us
    dot_general x1, matrix products, body(): jnp.dot(all_bands, lax.all_gather(rotation, 'ga', axis=0, tiled=True), pr...  34.3 us
    unnamed x15, local copies, waits for them, and re-layouts  28.3 us
    psum x1, blocking collectives, body(): squares = lax.psum(jnp.sum(rotated * rotated, axis=0), 'ga')  20.4 us
  transfers between devices with their start and end apart: 4, of which 4 were waited for; matrix products, arithmetic and copies ran while one was open for 6% of the time, Pallas kernels for 0%

profile of v1, /device:TPU:0, one launch (start us, length us, event | category | flops | bytes accessed | tf_op | source)
XLA Modules:
  0.0 442.4 jit_solution(8446889258284561667)
XLA Ops:
  7.2 0.0 all-gather.2.cloned.1.call-start
  7.2 0.7 all-gather.2.cloned.1.call-update
  7.9 0.5 collective-permute-start
  8.4 45.5 %collective-permute-done = bf16[1280,1536]{1,0:T(8,128)(2,1)S(1)} collective-permute-done((bf16[1280,1536]{1,0:T(8,128)(2,1)}, bf16[1280,1536]{1,0:T(8,128)(2,1)S(1)}, u32[]{:S(2)}, u32[]{:S(2)}) %collective-permute-start) | collective-permute-done | bytes 3932192 | tf_op jit(solution)/shard_map/ppermute | solution.py:12
  53.9 1.9 copy-done.1
  55.9 0.0 collective-permute-start.1
  55.9 45.2 %collective-permute-done.1 = bf16[1280,1536]{1,0:T(8,128)(2,1)} collective-permute-done((bf16[1280,1536]{1,0:T(8,128)(2,1)S(1)}, bf16[1280,1536]{1,0:T(8,128)(2,1)}, u32[]{:S(2)}, u32[]{:S(2)}) %collective-permute-start.1) | collective-permute-done | bytes 3932192 | tf_op jit(solution)/shard_map/ppermute | solution.py:12
  101.1 0.0 collective-permute-start.2
  101.1 45.4 %collective-permute-done.2 = bf16[1280,1536]{1,0:T(8,128)(2,1)} collective-permute-done((bf16[1280,1536]{1,0:T(8,128)(2,1)}, bf16[1280,1536]{1,0:T(8,128)(2,1)}, u32[]{:S(2)}, u32[]{:S(2)}) %collective-permute-start.2) | collective-permute-done | bytes 3932192 | tf_op jit(solution)/shard_map/ppermute | solution.py:12
  146.5 4.3 constant_dynamic-update-slice_fusion.7
  150.8 4.5 %constant_dynamic-update-slice_fusion.6 = bf16[1280,12288]{1,0:T(8,128)(2,1)} fusion(bf16[1280,12288]{1,0:T(8,128)(2,1)} %constant_dynamic-update-slice_fusion.7, bf16[1280,1536]{1,0:T(8,128)(2,1)} %collective-permute-done.1), kind=kLoop, calls=%fused_computation.10 | loop fusion | bytes 7864320
  155.3 4.4 constant_dynamic-update-slice_fusion.5
  159.7 0.0 copy-done
  159.7 2.2 constant_dynamic-update-slice_fusion.4
  161.9 4.3 constant_dynamic-update-slice_fusion.3
  166.2 4.4 constant_dynamic-update-slice_fusion.2
  170.7 0.0 copy-done.2
  170.7 2.2 constant_dynamic-update-slice_fusion.1
  172.9 2.2 constant_dynamic-update-slice_fusion
  175.0 199.6 %all-gather.2.cloned.1.call-done = bf16[6144,1536]{1,0:T(8,128)(2,1)} async-done(((bf16[768,1536]{1,0:T(8,128)(2,1)}), bf16[6144,1536]{1,0:T(8,128)(2,1)}) %all-gather.2.cloned.1.call-update) | async-done | bytes 18874384 | tf_op jit(solution)/shard_map/all_gather | solution.py:22
  374.7 34.3 %multiply_reduce_fusion = (f32[1536]{0:T(1024)S(1)}, f32[1280,1536]{1,0:T(8,128)}) fusion(bf16[6144,1536]{1,0:T(8,128)(2,1)} %all-gather.2.cloned.1.call-done, bf16[1280,12288]{1,0:T(8,128)(2,1)} %constant_dynamic-update-slice_fusion, s32[]{:T(128)S(6)} %select_n.14), kind=kOutput, calls=%fused_computation.3 | convolution fusion | flops 24163121152 | bytes 42473476 | tf_op jit(solution)/shard_map/dot_general | solution.py:20
  408.9 20.4 %psum.7 = f32[1536]{0:T(1024)S(1)} all-reduce(f32[1536]{0:T(1024)S(1)} %get-tuple-element.2), channel_id=1, replica_groups=mesh['ga'=8,'ba'=4] {'ga'}, use_global_device_ids=true, to_apply=%region_1.2 | all-reduce | flops 1536 | bytes 12288 | tf_op jit(solution)/shard_map/psum | solution.py:25
  429.4 0.0 copy-start.3
  429.4 6.2 %divide_convert_fusion = bf16[1280,1536]{1,0:T(8,128)(2,1)} fusion(f32[1280,1536]{1,0:T(8,128)} %get-tuple-element.3, f32[1536]{0:T(1024)S(1)} %add_sqrt_fusion), kind=kLoop, calls=%fused_computation.2 | loop fusion | flops 3932160 | bytes 11802624 | tf_op jit(solution)/shard_map/convert_element_type | solution.py:28
  (5 shorter events, 0.0 us)
Async XLA Ops:
  7.2 367.5 %all-gather.2.cloned.1.call-start = ((), (), s32[]{:S(2)}) async-start(), calls=%async_computation | async-start | bytes 21233664 | tf_op jit(solution)/shard_map/all_gather | solution.py:22
  7.9 46.0 %collective-permute-start = (bf16[1280,1536]{1,0:T(8,128)(2,1)}, bf16[1280,1536]{1,0:T(8,128)(2,1)S(1)}, u32[]{:S(2)}, u32[]{:S(2)}) collective-permute-start(bf16[1280,1536]{1,0:T(8,128)(2,1)} %param.2), channel_id=1, source_target_pairs={{0,1},{1,2},{2,3},{3,0},{4,5},{5,6},{6,7},{7,4},{8,9},{9,10},{10,1... | collective-permute-start | bytes 11796488 | tf_op jit(solution)/shard_map/ppermute | solution.py:12
  53.9 1.9 copy-start.1
  55.9 45.2 %collective-permute-start.1 = (bf16[1280,1536]{1,0:T(8,128)(2,1)S(1)}, bf16[1280,1536]{1,0:T(8,128)(2,1)}, u32[]{:S(2)}, u32[]{:S(2)}) collective-permute-start(bf16[1280,1536]{1,0:T(8,128)(2,1)S(1)} %collective-permute-done), channel_id=1, source_target_pairs={{0,1},{1,2},{2,3},{3,0},{4,5},{5,6},{6,7},{7,4},{8,9},{9,10},{10,1... | collective-permute-start | bytes 11796488 | tf_op jit(solution)/shard_map/ppermute | solution.py:12
  101.1 45.4 %collective-permute-start.2 = (bf16[1280,1536]{1,0:T(8,128)(2,1)}, bf16[1280,1536]{1,0:T(8,128)(2,1)}, u32[]{:S(2)}, u32[]{:S(2)}) collective-permute-start(bf16[1280,1536]{1,0:T(8,128)(2,1)} %collective-permute-done.1), channel_id=1, source_target_pairs={{0,1},{1,2},{2,3},{3,0},{4,5},{5,6},{6,7},{7,4},{8,9},{9,10},{10,1... | collective-permute-start | bytes 11796488 | tf_op jit(solution)/shard_map/ppermute | solution.py:12
  101.1 58.6 %copy-start = (bf16[1280,1536]{1,0:T(8,128)(2,1)S(1)}, bf16[1280,1536]{1,0:T(8,128)(2,1)}, u32[]{:S(2)}) copy-start(bf16[1280,1536]{1,0:T(8,128)(2,1)} %param.2) | copy-start | bytes 11796484
  150.8 19.9 %copy-start.2 = (bf16[1280,1536]{1,0:T(8,128)(2,1)S(1)}, bf16[1280,1536]{1,0:T(8,128)(2,1)}, u32[]{:S(2)}) copy-start(bf16[1280,1536]{1,0:T(8,128)(2,1)} %copy-done.1) | copy-start | bytes 11796484
  429.4 6.2 %copy-start.3 = (f32[1536]{0:T(1024)}, f32[1536]{0:T(1024)S(1)}, u32[]{:S(2)}) copy-start(f32[1536]{0:T(1024)S(1)} %add_sqrt_fusion) | copy-start | bytes 18436
Sparse Core Ops, SparseCore 0:
  9.5 365.1 all-gather.1
